TPU v7x, 32 devices: a whole 2x2x4 slice. The times are simulated.
32 devices in a mesh: row: 8 (over y, x, core), col: 4 (over z).
Axes of the slice: x: 2, y: 2, z: 4, core: 2. Of those that a mesh axis runs over, the one named last changes fastest.
Arguments:
- features: bfloat16 [32768, 512], P('col', 'row'), may hold values from -6 to 6
- weight_t: bfloat16 [512, 512], P(None, 'row'), may hold values from -0.25 to 0.25
- tiles: bfloat16 [8192, 128, 128], P(('row', 'col')), may hold values from -0.15625 to 0.15625
- coords: int32 [2, 8192], P(None, ('row', 'col')), may hold values from 0 to 63, as said below
- counts: int32 [32], P(('row', 'col')), may hold values from 32 to 256, as said below
Outputs:
- output: bfloat16 [32768, 512], P('row', 'col')
Inputs may be any that keep to these rules, and one draw needn't show every extreme that they name: coords[0] of a slot lies in 0 to 31 and coords[1] in 0 to 63; the live slots of one grid cell name distinct tiles. `counts`: some grid cell has all 256 slots live in every draw.
All inputs are finite; a program needn't handle non-finite values.
Results may differ from a plain program's by a relative error of at most 0.0095.
Values may be sent and summed in bfloat16 or wider, within the bound.
A program may use at most 128 MiB of HBM per device.

v0:
```python
import jax
import jax.numpy as jnp
from jax import lax
from jax.sharding import PartitionSpec as P

TROW = 32


def tile_apply(tiles, rows, cols, count, source):
    maxt = tiles.shape[0]
    tile = tiles.shape[1]
    width = source.shape[2]
    tcol_here = source.shape[0]
    group = min(32, maxt)
    offsets = jnp.arange(group, dtype=jnp.int32)
    col_lanes = jnp.arange(tcol_here, dtype=jnp.int32)
    row_lanes = jnp.arange(TROW, dtype=jnp.int32)

    def step(index, total):
        start = (index * group).astype(jnp.int32)
        block = lax.dynamic_slice_in_dim(tiles, start, group, 0)
        block_rows = lax.dynamic_slice_in_dim(rows, start, group, 0)
        block_cols = lax.dynamic_slice_in_dim(cols, start, group, 0)
        live = start + offsets < count
        pick_cols = (block_cols[:, None] == col_lanes[None, :]).astype(jnp.bfloat16)
        inputs = jnp.einsum(
            "gc,cjw->gjw", pick_cols, source, preferred_element_type=jnp.float32
        ).astype(jnp.bfloat16)
        prod = jnp.einsum("gij,gjw->giw", block, inputs, preferred_element_type=jnp.float32)
        place_rows = ((block_rows[:, None] == row_lanes[None, :]) & live[:, None]).astype(
            jnp.float32
        )
        added = jnp.einsum("gt,giw->tiw", place_rows, prod, precision=lax.Precision.HIGHEST)
        return total + added

    turns = (count + group - 1) // group
    total = lax.fori_loop(0, turns, step, jnp.zeros((TROW, tile, width), jnp.float32))
    return total.reshape(TROW * tile, width)


def body(features, weight_t, tiles, coords, counts):
    rows = coords[0]
    cols = coords[1]
    count = counts[0]
    tile = tiles.shape[1]
    tcol_here = features.shape[0] // tile
    panel, weight_full = (
        lax.all_gather(features, "row", axis=1, tiled=True),
        lax.all_gather(weight_t, "row", axis=1, tiled=True),
    )
    spread = tile_apply(tiles, rows, cols, count, panel.reshape(tcol_here, tile, panel.shape[1]))
    partial_value = lax.dot_general(
        spread,
        weight_full.astype(jnp.float32),
        (((1,), (1,)), ((), ())),
        precision=lax.Precision.HIGHEST,
    )
    summed = lax.psum_scatter(partial_value, "col", scatter_dimension=1, tiled=True)
    return summed.astype(jnp.bfloat16)


def solution(mesh):
    placed = (
        P("col", "row"),
        P(None, "row"),
        P(("row", "col"), None, None),
        P(None, ("row", "col")),
        P(("row", "col")),
    )
    return jax.shard_map(
        body, mesh=mesh, in_specs=placed, out_specs=P("row", "col"), check_vma=False
    )
```

profile of v0, /device:TPU:0, one launch (start us, length us, event | category | flops | bytes accessed | tf_op | source)
XLA Modules:
  0.0 516.9 jit_solution(8024863803451204911)
XLA Ops:
  6.5 0.0 all-gather.2.cloned.1.call-start
  6.5 0.7 all-gather.2.cloned.1.call-update
  7.3 0.0 reduce-scatter.2.cloned.1.call-start
  8.0 11.6 %all_gather.7 = bf16[512,512]{0,1:T(8,128)(2,1)S(1)} all-gather(bf16[512,64]{0,1:T(8,128)(2,1)} %param.8), channel_id=1, replica_groups=mesh['row'=8,'col'=4] {'row'}, dimensions={1}, use_global_device_ids=true | all-gather | bytes 589824 | tf_op jit(solution)/shard_map/all_gather | solution.py:49
  19.6 0.8 fusion.23
  20.4 45.9 %all-gather.2.cloned.1.call-done = bf16[8192,512]{0,1:T(8,128)(2,1)} async-done(((bf16[8192,64]{0,1:T(8,128)(2,1)}), bf16[8192,512]{0,1:T(8,128)(2,1)}) %all-gather.2.cloned.1.call-update) | async-done | bytes 8388624 | tf_op jit(solution)/shard_map/all_gather | solution.py:48
  66.2 12.0 %copy.7 = bf16[8192,512]{1,0:T(8,128)(2,1)} copy(bf16[8192,512]{0,1:T(8,128)(2,1)} %all-gather.2.cloned.1.call-done) | data formatting | bytes 16777216 | tf_op jit(solution)/shard_map/all_gather | solution.py:48
  78.2 4.3 broadcast_in_dim.13
  82.5 132.6 %while.13 = (s32[]{:T(128)}, f32[32,128,512]{2,0,1:T(8,128)}, s32[]{:T(128)}, s32[256]{0:T(256)S(1)}, s32[]{:T(128)}, /*index=5*/bf16[256,128,128]{2,1,0:T(8,128...) while((s32[]{:T(128)}, f32[32,128,512]{2,0,1:T(8,128)}, ...), condition=%wide.region_1.2_spmd.clone.clone, body=%wide.region_0.1_spmd.clone.clone.sunk | while | flops 1612713984 | bytes 51381240 | solution.py:37
  82.5 0.1 dynamic_slice.24
  82.6 13.4 %fusion.41 = bf16[32,128,512]{2,0,1:T(8,128)(2,1)S(1)} fusion(bf16[64,128,512]{2,1,0:T(8,128)(2,1)} %get-tuple-element.233, s32[32]{0:T(128)S(1)} %dynamic_slice.24), kind=kOutput, calls=%fused_computation.5.clone.1 | convolution fusion | flops 268437504 | bytes 12583040 | tf_op jit(solution)/shard_map/while/body/gc,cjw->gjw/dot_general | solution.py:26
  96.0 6.4 %fusion.42 = f32[32,128,512]{2,1,0:T(8,128)S(1)} fusion(bf16[32,128,512]{2,0,1:T(8,128)(2,1)S(1)} %fusion.41, bf16[256,128,128]{2,1,0:T(8,128)(2,1)} %get-tuple-element.231, s32[]{:T(128)S(6)} %select_n.15), kind=kOutput, calls=%fused_computation.7.clone.1 | convolution fusion | flops 536870912 | bytes 13631492 | tf_op jit(solution)/shard_map/while/body/gij,gjw->giw/dot_general | solution.py:29
  102.3 0.1 dynamic_slice.25
  102.4 0.7 fusion.43
  103.1 12.6 %fusion.44 = f32[32,128,512]{2,0,1:T(8,128)} fusion(f32[32,128,512]{2,0,1:T(8,128)} %get-tuple-element.215, f32[32,128,512]{2,1,0:T(8,128)S(1)} %fusion.42, s32[32]{0:T(128)S(1)} %dynamic_slice.25, pred[32]{0:T(512)(128)(4,1)S(1)} %fusion.43), kind=kOutput, calls=%fused_computation.8.clone.1 | convolution fusion | flops 807405568 | bytes 25165984 | tf_op jit(solution)/shard_map/while/body/gt,giw->tiw/dot_general | solution.py:33
  115.7 0.1 dynamic_slice.24
  115.7 13.4 %fusion.41 = bf16[32,128,512]{2,0,1:T(8,128)(2,1)S(1)} fusion(bf16[64,128,512]{2,1,0:T(8,128)(2,1)} %get-tuple-element.233, s32[32]{0:T(128)S(1)} %dynamic_slice.24), kind=kOutput, calls=%fused_computation.5.clone.1 | convolution fusion | flops 268437504 | bytes 12583040 | tf_op jit(solution)/shard_map/while/body/gc,cjw->gjw/dot_general | solution.py:26
  129.1 6.4 %fusion.42 = f32[32,128,512]{2,1,0:T(8,128)S(1)} fusion(bf16[32,128,512]{2,0,1:T(8,128)(2,1)S(1)} %fusion.41, bf16[256,128,128]{2,1,0:T(8,128)(2,1)} %get-tuple-element.231, s32[]{:T(128)S(6)} %select_n.15), kind=kOutput, calls=%fused_computation.7.clone.1 | convolution fusion | flops 536870912 | bytes 13631492 | tf_op jit(solution)/shard_map/while/body/gij,gjw->giw/dot_general | solution.py:29
  135.5 0.1 dynamic_slice.25
  135.5 0.7 fusion.43
  136.2 12.6 %fusion.44 = f32[32,128,512]{2,0,1:T(8,128)} fusion(f32[32,128,512]{2,0,1:T(8,128)} %get-tuple-element.215, f32[32,128,512]{2,1,0:T(8,128)S(1)} %fusion.42, s32[32]{0:T(128)S(1)} %dynamic_slice.25, pred[32]{0:T(512)(128)(4,1)S(1)} %fusion.43), kind=kOutput, calls=%fused_computation.8.clone.1 | convolution fusion | flops 807405568 | bytes 25165984 | tf_op jit(solution)/shard_map/while/body/gt,giw->tiw/dot_general | solution.py:33
  148.8 0.1 dynamic_slice.24
  148.9 13.4 %fusion.41 = bf16[32,128,512]{2,0,1:T(8,128)(2,1)S(1)} fusion(bf16[64,128,512]{2,1,0:T(8,128)(2,1)} %get-tuple-element.233, s32[32]{0:T(128)S(1)} %dynamic_slice.24), kind=kOutput, calls=%fused_computation.5.clone.1 | convolution fusion | flops 268437504 | bytes 12583040 | tf_op jit(solution)/shard_map/while/body/gc,cjw->gjw/dot_general | solution.py:26
  162.3 6.4 %fusion.42 = f32[32,128,512]{2,1,0:T(8,128)S(1)} fusion(bf16[32,128,512]{2,0,1:T(8,128)(2,1)S(1)} %fusion.41, bf16[256,128,128]{2,1,0:T(8,128)(2,1)} %get-tuple-element.231, s32[]{:T(128)S(6)} %select_n.15), kind=kOutput, calls=%fused_computation.7.clone.1 | convolution fusion | flops 536870912 | bytes 13631492 | tf_op jit(solution)/shard_map/while/body/gij,gjw->giw/dot_general | solution.py:29
  168.6 0.1 dynamic_slice.25
  168.7 0.7 fusion.43
  169.4 12.6 %fusion.44 = f32[32,128,512]{2,0,1:T(8,128)} fusion(f32[32,128,512]{2,0,1:T(8,128)} %get-tuple-element.215, f32[32,128,512]{2,1,0:T(8,128)S(1)} %fusion.42, s32[32]{0:T(128)S(1)} %dynamic_slice.25, pred[32]{0:T(512)(128)(4,1)S(1)} %fusion.43), kind=kOutput, calls=%fused_computation.8.clone.1 | convolution fusion | flops 807405568 | bytes 25165984 | tf_op jit(solution)/shard_map/while/body/gt,giw->tiw/dot_general | solution.py:33
  182.0 0.1 dynamic_slice.24
  182.0 13.4 %fusion.41 = bf16[32,128,512]{2,0,1:T(8,128)(2,1)S(1)} fusion(bf16[64,128,512]{2,1,0:T(8,128)(2,1)} %get-tuple-element.233, s32[32]{0:T(128)S(1)} %dynamic_slice.24), kind=kOutput, calls=%fused_computation.5.clone.1 | convolution fusion | flops 268437504 | bytes 12583040 | tf_op jit(solution)/shard_map/while/body/gc,cjw->gjw/dot_general | solution.py:26
  195.4 6.4 %fusion.42 = f32[32,128,512]{2,1,0:T(8,128)S(1)} fusion(bf16[32,128,512]{2,0,1:T(8,128)(2,1)S(1)} %fusion.41, bf16[256,128,128]{2,1,0:T(8,128)(2,1)} %get-tuple-element.231, s32[]{:T(128)S(6)} %select_n.15), kind=kOutput, calls=%fused_computation.7.clone.1 | convolution fusion | flops 536870912 | bytes 13631492 | tf_op jit(solution)/shard_map/while/body/gij,gjw->giw/dot_general | solution.py:29
  201.8 0.1 dynamic_slice.25
  201.9 0.7 fusion.43
  202.5 12.6 %fusion.44 = f32[32,128,512]{2,0,1:T(8,128)} fusion(f32[32,128,512]{2,0,1:T(8,128)} %get-tuple-element.215, f32[32,128,512]{2,1,0:T(8,128)S(1)} %fusion.42, s32[32]{0:T(128)S(1)} %dynamic_slice.25, pred[32]{0:T(512)(128)(4,1)S(1)} %fusion.43), kind=kOutput, calls=%fused_computation.8.clone.1 | convolution fusion | flops 807405568 | bytes 25165984 | tf_op jit(solution)/shard_map/while/body/gt,giw->tiw/dot_general | solution.py:33
  215.1 8.2 %copy.8 = f32[32,128,512]{2,1,0:T(8,128)S(1)} copy(f32[32,128,512]{2,0,1:T(8,128)} %get-tuple-element.88) | data formatting | bytes 16777216 | tf_op jit(solution)/shard_map/while | solution.py:37
  223.4 8.9 %fusion.24 = f32[4096,512]{1,0:T(8,128)} fusion(f32[4096,512]{1,0:T(8,128)S(1)} %bitcast.19, bf16[512,512]{0,1:T(8,128)(2,1)S(1)} %all_gather.7), kind=kOutput, calls=%fused_computation.22 | convolution fusion | flops 12884901888 | bytes 17301504 | tf_op jit(solution)/shard_map/dot_general | solution.py:52
  232.3 0.0 reduce-scatter.2.cloned.1.call-update
  232.3 275.1 %reduce-scatter.2.cloned.1.call-done = f32[4096,128]{1,0:T(8,128)} async-done(((f32[4096,512]{1,0:T(8,128)}), f32[4096,128]{1,0:T(8,128)}) %reduce-scatter.2.cloned.1.call-update) | async-done | bytes 2097168 | tf_op jit(solution)/shard_map/reduce_scatter | solution.py:58
  507.4 2.7 convert_element_type.12
Async XLA Ops:
  6.5 59.7 %all-gather.2.cloned.1.call-start = ((), (), s32[]{:S(2)}) async-start(), calls=%async_computation.1 | async-start | bytes 9437184 | tf_op jit(solution)/shard_map/all_gather | solution.py:48
  7.3 500.1 %reduce-scatter.2.cloned.1.call-start = ((), (), s32[]{:S(2)}) async-start(), calls=%async_computation.2 | async-start | bytes 10485760 | tf_op jit(solution)/shard_map/reduce_scatter | solution.py:58
Sparse Core Ops, SparseCore 0:
  9.2 56.9 all-gather.1
  232.4 274.9 reduce-scatter.1
where the time goes:
time: 518 us; the launch traced here: 517 us
  waiting for transfers between devices  322 us (62%)
  matrix products  138 us (27%)
  local copies, waits for them, and re-layouts  25.9 us (5%)
  between operations  14.1 us (3%)
  blocking collectives  11.6 us (2%)
  other arithmetic  5.26 us (1%)
    reduce_scatter x1, waiting for transfers between devices, body(): lax.psum_scatter(partial_value, 'col', scatter_dimension=1, tiled=True)  275 us
    dot_general x4, matrix products, step(): jnp.einsum('gc,cjw->gjw', pick_cols, source, preferred_element_type=jnp.f...  53.5 us
    dot_general x4, matrix products, step(): jnp.einsum('gt,giw->tiw', place_rows, prod, precision=lax.Precision.HIGHEST)  50.4 us
    all_gather x1, waiting for transfers between devices, body(): lax.all_gather(features, 'row', axis=1, tiled=True)  45.9 us
    dot_general x4, matrix products, step(): jnp.einsum('gij,gjw->giw', block, inputs, preferred_element_type=jnp.floa...  25.4 us
    all_gather x1, local copies, waits for them, and re-layouts, body(): lax.all_gather(features, 'row', axis=1, tiled=True)  12 us
    all_gather x1, blocking collectives, body(): lax.all_gather(weight_t, 'row', axis=1, tiled=True)  11.6 us
  transfers between devices with their start and end apart: 2, of which 2 were waited for; matrix products, arithmetic and copies ran while one was open for 0% of the time, Pallas kernels for 0%

commit v1 on v0

--- a/solution.py
+++ b/solution.py
@@ -4,6 +4,12 @@
 from jax.sharding import PartitionSpec as P
 
 TROW = 32
+
+
+def gather_blocks(x, axis, dim):
+    blocks = lax.all_gather(x, axis, axis=0, tiled=False)
+    out = jnp.concatenate(blocks, axis=dim)
+    return out
 
 
 def tile_apply(tiles, rows, cols, count, source):
@@ -45,7 +51,7 @@
     tile = tiles.shape[1]
     tcol_here = features.shape[0] // tile
     panel, weight_full = (
-        lax.all_gather(features, "row", axis=1, tiled=True),
+        gather_blocks(features, "row", 1),
         lax.all_gather(weight_t, "row", axis=1, tiled=True),
     )
     spread = tile_apply(tiles, rows, cols, count, panel.reshape(tcol_here, tile, panel.shape[1]))

time: 518 us -> 536 us (1.035)
  local copies, waits for them, and re-layouts: 25.9 us -> 43.5 us
    unnamed x0 -> x2, local copies, waits for them, and re-layouts: none -> 22 us
where the time goes in v1:
time: 536 us; the launch traced here: 535 us
  waiting for transfers between devices  322 us (60%)
  matrix products  138 us (26%)
  local copies, waits for them, and re-layouts  43.5 us (8%)
  between operations  14.1 us (3%)
  blocking collectives  11.6 us (2%)
    reduce_scatter x1, waiting for transfers between devices, body(): lax.psum_scatter(partial_value, 'col', scatter_dimension=1, tiled=True)  275 us
    dot_general x4, matrix products, step(): jnp.einsum('gc,cjw->gjw', pick_cols, source, preferred_element_type=jnp.f...  53.5 us
    dot_general x4, matrix products, step(): jnp.einsum('gt,giw->tiw', place_rows, prod, precision=lax.Precision.HIGHEST)  50.6 us
    all_gather x1, waiting for transfers between devices, gather_blocks(): blocks = lax.all_gather(x, axis, axis=0, tiled=False)  45.9 us
    dot_general x4, matrix products, step(): jnp.einsum('gij,gjw->giw', block, inputs, preferred_element_type=jnp.floa...  25.4 us
    unnamed x2, local copies, waits for them, and re-layouts  22 us
    all_gather x1, blocking collectives, body(): lax.all_gather(weight_t, 'row', axis=1, tiled=True)  11.6 us
  transfers between devices with their start and end apart: 2, of which 2 were waited for; matrix products, arithmetic and copies ran while one was open for 0% of the time, Pallas kernels for 0%

profile of v1, /device:TPU:0, one launch (start us, length us, event | category | flops | bytes accessed | tf_op | source)
XLA Modules:
  0.0 534.9 jit_solution(13196409784644488448)
XLA Ops:
  6.5 0.0 all-gather.3.cloned.1.call-start
  6.5 0.7 all-gather.3.cloned.1.call-update
  7.3 0.0 reduce-scatter.2.cloned.1.call-start
  8.0 11.6 %all_gather.11 = bf16[512,512]{0,1:T(8,128)(2,1)S(1)} all-gather(bf16[512,64]{0,1:T(8,128)(2,1)} %param.8), channel_id=1, replica_groups=mesh['row'=8,'col'=4] {'row'}, dimensions={1}, use_global_device_ids=true | all-gather | bytes 589824 | tf_op jit(solution)/shard_map/all_gather | solution.py:55
  19.6 0.8 fusion.23
  20.4 45.9 %all-gather.3.cloned.1.call-done = bf16[65536,64]{0,1:T(8,128)(2,1)} async-done(((bf16[8192,64]{0,1:T(8,128)(2,1)}), bf16[65536,64]{0,1:T(8,128)(2,1)}) %all-gather.3.cloned.1.call-update) | async-done | bytes 8388624 | tf_op jit(solution)/shard_map/all_gather | solution.py:10
  66.3 7.6 %copy.24 = bf16[8,8,8,8192]{3,2,0,1:T(8,128)(2,1)} copy(bf16[8,8,8,8192]{3,2,1,0:T(8,128)(2,1)} %bitcast.30) | data formatting | bytes 16777216 | tf_op jit(solution)/shard_map/all_gather | solution.py:10
  73.9 9.3 %copy.14 = bf16[64,8,64,128]{3,2,1,0:T(8,128)(2,1)} copy(bf16[64,8,64,128]{3,1,2,0:T(8,128)(2,1)} %bitcast.28) | data formatting | bytes 16777216
  83.2 12.7 %copy.8 = bf16[64,128,512]{2,1,0:T(8,128)(2,1)} copy(bf16[64,128,512]{1,0,2:T(8,128)(2,1)} %bitcast.29) | data formatting | bytes 16777216
  95.8 4.3 broadcast_in_dim.13
  100.1 132.8 %while.13 = (s32[]{:T(128)}, f32[32,128,512]{2,0,1:T(8,128)}, s32[]{:T(128)}, s32[256]{0:T(256)S(1)}, s32[]{:T(128)}, /*index=5*/bf16[256,128,128]{2,1,0:T(8,128...) while((s32[]{:T(128)}, f32[32,128,512]{2,0,1:T(8,128)}, ...), condition=%wide.region_1.2_spmd.clone.clone, body=%wide.region_0.1_spmd.clone.clone.sunk | while | flops 1612713984 | bytes 51381240 | solution.py:43
  100.1 0.1 dynamic_slice.24
  100.2 13.4 %fusion.41 = bf16[32,128,512]{2,0,1:T(8,128)(2,1)S(1)} fusion(bf16[64,128,512]{2,1,0:T(8,128)(2,1)} %get-tuple-element.241, s32[32]{0:T(128)S(1)} %dynamic_slice.24), kind=kOutput, calls=%fused_computation.5.clone.1 | convolution fusion | flops 268437504 | bytes 12583040 | tf_op jit(solution)/shard_map/while/body/gc,cjw->gjw/dot_general | solution.py:32
  113.6 6.4 %fusion.42 = f32[32,128,512]{2,1,0:T(8,128)S(1)} fusion(bf16[32,128,512]{2,0,1:T(8,128)(2,1)S(1)} %fusion.41, bf16[256,128,128]{2,1,0:T(8,128)(2,1)} %get-tuple-element.239, s32[]{:T(128)S(6)} %select_n.15), kind=kOutput, calls=%fused_computation.7.clone.1 | convolution fusion | flops 536870912 | bytes 13631492 | tf_op jit(solution)/shard_map/while/body/gij,gjw->giw/dot_general | solution.py:35
  119.9 0.1 dynamic_slice.25
  120.0 0.7 fusion.43
  120.7 12.7 %fusion.44 = f32[32,128,512]{2,0,1:T(8,128)} fusion(f32[32,128,512]{2,0,1:T(8,128)} %get-tuple-element.223, f32[32,128,512]{2,1,0:T(8,128)S(1)} %fusion.42, s32[32]{0:T(128)S(1)} %dynamic_slice.25, pred[32]{0:T(512)(128)(4,1)S(1)} %fusion.43), kind=kOutput, calls=%fused_computation.8.clone.1 | convolution fusion | flops 807405568 | bytes 25165984 | tf_op jit(solution)/shard_map/while/body/gt,giw->tiw/dot_general | solution.py:39
  133.3 0.1 dynamic_slice.24
  133.4 13.4 %fusion.41 = bf16[32,128,512]{2,0,1:T(8,128)(2,1)S(1)} fusion(bf16[64,128,512]{2,1,0:T(8,128)(2,1)} %get-tuple-element.241, s32[32]{0:T(128)S(1)} %dynamic_slice.24), kind=kOutput, calls=%fused_computation.5.clone.1 | convolution fusion | flops 268437504 | bytes 12583040 | tf_op jit(solution)/shard_map/while/body/gc,cjw->gjw/dot_general | solution.py:32
  146.8 6.4 %fusion.42 = f32[32,128,512]{2,1,0:T(8,128)S(1)} fusion(bf16[32,128,512]{2,0,1:T(8,128)(2,1)S(1)} %fusion.41, bf16[256,128,128]{2,1,0:T(8,128)(2,1)} %get-tuple-element.239, s32[]{:T(128)S(6)} %select_n.15), kind=kOutput, calls=%fused_computation.7.clone.1 | convolution fusion | flops 536870912 | bytes 13631492 | tf_op jit(solution)/shard_map/while/body/gij,gjw->giw/dot_general | solution.py:35
  153.1 0.1 dynamic_slice.25
  153.2 0.7 fusion.43
  153.9 12.7 %fusion.44 = f32[32,128,512]{2,0,1:T(8,128)} fusion(f32[32,128,512]{2,0,1:T(8,128)} %get-tuple-element.223, f32[32,128,512]{2,1,0:T(8,128)S(1)} %fusion.42, s32[32]{0:T(128)S(1)} %dynamic_slice.25, pred[32]{0:T(512)(128)(4,1)S(1)} %fusion.43), kind=kOutput, calls=%fused_computation.8.clone.1 | convolution fusion | flops 807405568 | bytes 25165984 | tf_op jit(solution)/shard_map/while/body/gt,giw->tiw/dot_general | solution.py:39
  166.5 0.1 dynamic_slice.24
  166.6 13.4 %fusion.41 = bf16[32,128,512]{2,0,1:T(8,128)(2,1)S(1)} fusion(bf16[64,128,512]{2,1,0:T(8,128)(2,1)} %get-tuple-element.241, s32[32]{0:T(128)S(1)} %dynamic_slice.24), kind=kOutput, calls=%fused_computation.5.clone.1 | convolution fusion | flops 268437504 | bytes 12583040 | tf_op jit(solution)/shard_map/while/body/gc,cjw->gjw/dot_general | solution.py:32
  180.0 6.4 %fusion.42 = f32[32,128,512]{2,1,0:T(8,128)S(1)} fusion(bf16[32,128,512]{2,0,1:T(8,128)(2,1)S(1)} %fusion.41, bf16[256,128,128]{2,1,0:T(8,128)(2,1)} %get-tuple-element.239, s32[]{:T(128)S(6)} %select_n.15), kind=kOutput, calls=%fused_computation.7.clone.1 | convolution fusion | flops 536870912 | bytes 13631492 | tf_op jit(solution)/shard_map/while/body/gij,gjw->giw/dot_general | solution.py:35
  186.3 0.1 dynamic_slice.25
  186.4 0.7 fusion.43
  187.1 12.7 %fusion.44 = f32[32,128,512]{2,0,1:T(8,128)} fusion(f32[32,128,512]{2,0,1:T(8,128)} %get-tuple-element.223, f32[32,128,512]{2,1,0:T(8,128)S(1)} %fusion.42, s32[32]{0:T(128)S(1)} %dynamic_slice.25, pred[32]{0:T(512)(128)(4,1)S(1)} %fusion.43), kind=kOutput, calls=%fused_computation.8.clone.1 | convolution fusion | flops 807405568 | bytes 25165984 | tf_op jit(solution)/shard_map/while/body/gt,giw->tiw/dot_general | solution.py:39
  199.7 0.1 dynamic_slice.24
  199.8 13.4 %fusion.41 = bf16[32,128,512]{2,0,1:T(8,128)(2,1)S(1)} fusion(bf16[64,128,512]{2,1,0:T(8,128)(2,1)} %get-tuple-element.241, s32[32]{0:T(128)S(1)} %dynamic_slice.24), kind=kOutput, calls=%fused_computation.5.clone.1 | convolution fusion | flops 268437504 | bytes 12583040 | tf_op jit(solution)/shard_map/while/body/gc,cjw->gjw/dot_general | solution.py:32
  213.2 6.4 %fusion.42 = f32[32,128,512]{2,1,0:T(8,128)S(1)} fusion(bf16[32,128,512]{2,0,1:T(8,128)(2,1)S(1)} %fusion.41, bf16[256,128,128]{2,1,0:T(8,128)(2,1)} %get-tuple-element.239, s32[]{:T(128)S(6)} %select_n.15), kind=kOutput, calls=%fused_computation.7.clone.1 | convolution fusion | flops 536870912 | bytes 13631492 | tf_op jit(solution)/shard_map/while/body/gij,gjw->giw/dot_general | solution.py:35
  219.5 0.1 dynamic_slice.25
  219.6 0.7 fusion.43
  220.3 12.7 %fusion.44 = f32[32,128,512]{2,0,1:T(8,128)} fusion(f32[32,128,512]{2,0,1:T(8,128)} %get-tuple-element.223, f32[32,128,512]{2,1,0:T(8,128)S(1)} %fusion.42, s32[32]{0:T(128)S(1)} %dynamic_slice.25, pred[32]{0:T(512)(128)(4,1)S(1)} %fusion.43), kind=kOutput, calls=%fused_computation.8.clone.1 | convolution fusion | flops 807405568 | bytes 25165984 | tf_op jit(solution)/shard_map/while/body/gt,giw->tiw/dot_general | solution.py:39
  232.9 8.2 %copy.9 = f32[32,128,512]{2,1,0:T(8,128)S(1)} copy(f32[32,128,512]{2,0,1:T(8,128)} %get-tuple-element.88) | data formatting | bytes 16777216 | tf_op jit(solution)/shard_map/while | solution.py:43
  241.2 8.9 %fusion.24 = f32[4096,512]{1,0:T(8,128)} fusion(f32[4096,512]{1,0:T(8,128)S(1)} %bitcast.27, bf16[512,512]{0,1:T(8,128)(2,1)S(1)} %all_gather.11), kind=kOutput, calls=%fused_computation.23 | convolution fusion | flops 12884901888 | bytes 17301504 | tf_op jit(solution)/shard_map/dot_general | solution.py:58
  250.1 0.0 reduce-scatter.2.cloned.1.call-update
  250.1 275.3 %reduce-scatter.2.cloned.1.call-done = f32[4096,128]{1,0:T(8,128)} async-done(((f32[4096,512]{1,0:T(8,128)}), f32[4096,128]{1,0:T(8,128)}) %reduce-scatter.2.cloned.1.call-update) | async-done | bytes 2097168 | tf_op jit(solution)/shard_map/reduce_scatter | solution.py:64
  525.4 2.7 convert_element_type.12
Async XLA Ops:
  6.5 59.7 %all-gather.3.cloned.1.call-start = ((), (), s32[]{:S(2)}) async-start(), calls=%async_computation.2 | async-start | bytes 9437184 | tf_op jit(solution)/shard_map/all_gather | solution.py:10
  7.3 518.1 %reduce-scatter.2.cloned.1.call-start = ((), (), s32[]{:S(2)}) async-start(), calls=%async_computation.1 | async-start | bytes 10485760 | tf_op jit(solution)/shard_map/reduce_scatter | solution.py:64
Sparse Core Ops, SparseCore 0:
  9.2 56.9 all-gather.2
  250.2 275.1 reduce-scatter.1
